TPU v7x, 32 devices: a whole 2x2x4 slice. The times are simulated.
32 devices in a mesh: fsdp: 8 (over z, y), cols: 4 (over x, core).
Axes of the slice: x: 2, y: 2, z: 4, core: 2. Of those that a mesh axis runs over, the one named last changes fastest.
Arguments:
- train_gate: bfloat16 [3584, 14336], P('fsdp', 'cols'), may hold values from -0.09375 to 0.09375
- low_gate: bfloat16 [3584, 16], P('fsdp'), may hold values from -0.09375 to 0.09375
- high_gate: bfloat16 [16, 14336], P(None, 'cols'), may hold values from -1.5 to 1.5
- train_up: bfloat16 [3584, 14336], P('fsdp', 'cols'), may hold values from -0.09375 to 0.09375
- low_up: bfloat16 [3584, 16], P('fsdp'), may hold values from -0.09375 to 0.09375
- high_up: bfloat16 [16, 14336], P(None, 'cols'), may hold values from -1.5 to 1.5
- train_down: bfloat16 [14336, 3584], P('cols', 'fsdp'), may hold values from -0.046875 to 0.046875
- low_down: bfloat16 [14336, 16], P('cols'), may hold values from -0.046875 to 0.046875
- high_down: bfloat16 [16, 3584], P(None, 'fsdp'), may hold values from -1.5 to 1.5
- norm_train: float32 [3584], P(('fsdp', 'cols')), may hold values from 0.25 to 1.75
- norm_step: float32 [3584], P(('fsdp', 'cols')), may hold values from -0.3 to 0.3
Outputs:
- serving_gate: bfloat16 [3584, 14336], P(None, 'cols')
- serving_up: bfloat16 [3584, 14336], P(None, 'cols')
- serving_down: bfloat16 [14336, 3584], P('cols')
- serve_norm: bfloat16 [3584], replicated
All inputs are finite; a program needn't handle non-finite values.
Results may differ from a plain program's by a relative error of at most 0.001.
Values may be sent and summed in bfloat16 or wider, within the bound.
A program may use at most 256 MiB of HBM per device.

v0:
```python
import jax
import jax.numpy as jnp
from jax import lax
from jax.sharding import PartitionSpec as P

mix_rate = 1.0


def per_device(
    train_gate,
    low_gate,
    high_gate,
    train_up,
    low_up,
    high_up,
    train_down,
    low_down,
    high_down,
    norm_train,
    norm_step,
):
    moved_gate, moved_up, moved_down, factor_gate, factor_up, factor_down = (
        lax.all_gather(train_gate, "fsdp", axis=0, tiled=True),
        lax.all_gather(train_up, "fsdp", axis=0, tiled=True),
        lax.all_gather(train_down, "fsdp", axis=1, tiled=True),
        lax.all_gather(low_gate, "fsdp", axis=0, tiled=True),
        lax.all_gather(low_up, "fsdp", axis=0, tiled=True),
        lax.all_gather(high_down, "fsdp", axis=1, tiled=True),
    )
    whole_gate = moved_gate.astype(jnp.float32) + mix_rate * jnp.dot(
        factor_gate, high_gate, preferred_element_type=jnp.float32
    )
    serving_gate = whole_gate.astype(jnp.bfloat16)
    whole_up = moved_up.astype(jnp.float32) + mix_rate * jnp.dot(
        factor_up, high_up, preferred_element_type=jnp.float32
    )
    serving_up = whole_up.astype(jnp.bfloat16)
    whole_down = moved_down.astype(jnp.float32) + mix_rate * jnp.dot(
        low_down, factor_down, preferred_element_type=jnp.float32
    )
    serving_down = whole_down.astype(jnp.bfloat16)
    serve_norm = lax.all_gather(
        (norm_train + norm_step).astype(jnp.bfloat16), ("fsdp", "cols"), axis=0, tiled=True
    )
    return (serving_gate, serving_up, serving_down, serve_norm)


def solution(mesh):
    return jax.shard_map(
        per_device,
        mesh=mesh,
        in_specs=(
            P("fsdp", "cols"),
            P("fsdp", None),
            P(None, "cols"),
            P("fsdp", "cols"),
            P("fsdp", None),
            P(None, "cols"),
            P("cols", "fsdp"),
            P("cols", None),
            P(None, "fsdp"),
            P(("fsdp", "cols")),
            P(("fsdp", "cols")),
        ),
        out_specs=(P(None, "cols"), P(None, "cols"), P("cols", None), P()),
        check_vma=False,
    )
```

profile of v0, /device:TPU:0, one launch (start us, length us, event | category | flops | bytes accessed | tf_op | source)
XLA Modules:
  0.0 1519.4 jit_solution(11582905824135351410)
XLA Ops:
  7.2 0.0 copy-start
  7.2 0.0 all-gather.11.cloned.1.call-start
  7.2 0.7 all-gather.11.cloned.1.call-update
  7.9 0.0 all-gather.7.cloned.1.call-start
  8.0 0.7 all-gather.7.cloned.1.call-update
  8.7 0.0 all-gather.9.cloned.1.call-start
  8.7 0.7 all-gather.9.cloned.1.call-update
  9.4 70.0 %all-gather = bf16[8,448,16]{1,2,0:T(8,128)(2,1)S(1)} all-gather(bf16[1,448,16]{1,2,0:T(8,128)(2,1)} %bitcast.17), channel_id=1, replica_groups=mesh['fsdp'=8,'cols'=4] {'fsdp'}, dimensions={0}, use_global_device_ids=true | all-gather | bytes 129024 | tf_op jit(solution)/shard_map/all_gather | solution.py:26
  79.5 0.1 copy.20
  79.5 0.2 reshape.11
  79.7 43.9 %all-gather.1 = bf16[8,448,16]{1,2,0:T(8,128)(2,1)S(1)} all-gather(bf16[1,448,16]{1,2,0:T(8,128)(2,1)} %bitcast.18), channel_id=1, replica_groups=mesh['fsdp'=8,'cols'=4] {'fsdp'}, dimensions={0}, use_global_device_ids=true | all-gather | bytes 129024 | tf_op jit(solution)/shard_map/all_gather | solution.py:27
  123.6 0.1 copy.21
  123.7 0.2 reshape.13
  123.9 48.2 %all-gather.2 = bf16[8,448,16]{1,2,0:T(8,128)(2,1)S(1)} all-gather(bf16[1,448,16]{1,2,0:T(8,128)(2,1)} %bitcast.19), channel_id=1, replica_groups=mesh['fsdp'=8,'cols'=4] {'fsdp'}, dimensions={0}, use_global_device_ids=true | all-gather | bytes 129024 | tf_op jit(solution)/shard_map/all_gather | solution.py:28
  172.1 0.1 copy.23
  172.2 0.2 reshape.15
  172.3 0.7 add_convert_fusion.3
  173.0 0.2 dynamic-update-slice
  173.2 64.3 %all-reduce = bf16[3584]{0:T(1024)(128)(2,1)} all-reduce(bf16[3584]{0:T(1024)(128)(2,1)S(1)} %dynamic-update-slice), channel_id=1, replica_groups=mesh['fsdp'=8,'cols'=4] {'fsdp','cols'}, use_global_device_ids=true, to_apply=%add | all-reduce | flops 3584 | bytes 14336
  237.5 273.3 %all-gather.11.cloned.1.call-done = bf16[3584,3584]{0,1:T(8,128)(2,1)} async-done(((bf16[3584,448]{0,1:T(8,128)(2,1)}), bf16[3584,3584]{0,1:T(8,128)(2,1)}) %all-gather.11.cloned.1.call-update) | async-done | bytes 25690128 | tf_op jit(solution)/shard_map/all_gather | solution.py:25
  510.8 31.9 %copy.22 = bf16[3584,3584]{1,0:T(8,128)(2,1)} copy(bf16[3584,3584]{0,1:T(8,128)(2,1)} %all-gather.11.cloned.1.call-done) | data formatting | bytes 51380224 | tf_op jit(solution)/shard_map/all_gather | solution.py:25
  542.7 0.0 copy-done
  542.7 0.0 copy-start.2
  542.7 18.9 %add_convert_fusion = bf16[3584,3584]{1,0:T(8,128)(2,1)} fusion(bf16[3584,3584]{1,0:T(8,128)(2,1)} %copy.22, bf16[3584,16]{0,1:T(8,128)(2,1)S(1)} %copy-done, bf16[3584,16]{0,1:T(8,128)(2,1)S(1)} %reshape.15), kind=kOutput, calls=%fused_computation | convolution fusion | flops 449576960 | bytes 51609600 | tf_op jit(solution)/shard_map/dot_general | solution.py:38
  561.6 0.0 copy-start.3
  561.6 440.7 %all-gather.7.cloned.1.call-done = bf16[3584,3584]{1,0:T(8,128)(2,1)} async-done(((bf16[448,3584]{1,0:T(8,128)(2,1)}), bf16[3584,3584]{1,0:T(8,128)(2,1)}) %all-gather.7.cloned.1.call-update) | async-done | bytes 25690128 | tf_op jit(solution)/shard_map/all_gather | solution.py:23
  1002.4 0.0 copy-done.2
  1002.4 18.9 %add_convert_fusion.2 = bf16[3584,3584]{1,0:T(8,128)(2,1)} fusion(bf16[3584,3584]{1,0:T(8,128)(2,1)} %all-gather.7.cloned.1.call-done, bf16[3584,16]{0,1:T(8,128)(2,1)S(1)} %reshape.11, bf16[16,3584]{1,0:T(8,128)(2,1)S(1)} %copy-done.2), kind=kOutput, calls=%fused_computation.2 | convolution fusion | flops 449576960 | bytes 51609600 | tf_op jit(solution)/shard_map/dot_general | solution.py:30
  1021.3 472.9 %all-gather.9.cloned.1.call-done = bf16[3584,3584]{1,0:T(8,128)(2,1)} async-done(((bf16[448,3584]{1,0:T(8,128)(2,1)}), bf16[3584,3584]{1,0:T(8,128)(2,1)}) %all-gather.9.cloned.1.call-update) | async-done | bytes 25690128 | tf_op jit(solution)/shard_map/all_gather | solution.py:24
  1494.1 0.0 copy-done.3
  1494.1 18.7 %add_convert_fusion.1 = bf16[3584,3584]{1,0:T(8,128)(2,1)} fusion(bf16[3584,3584]{1,0:T(8,128)(2,1)} %all-gather.9.cloned.1.call-done, bf16[3584,16]{0,1:T(8,128)(2,1)S(1)} %reshape.13, bf16[16,3584]{1,0:T(8,128)(2,1)S(1)} %copy-done.3), kind=kOutput, calls=%fused_computation.1 | convolution fusion | flops 449576960 | bytes 51609600 | tf_op jit(solution)/shard_map/dot_general | solution.py:34
  1512.8 0.0 copy-done.1
  (2 shorter events, 0.0 us)
Async XLA Ops:
  7.2 535.6 %copy-start = (bf16[3584,16]{0,1:T(8,128)(2,1)S(1)}, bf16[3584,16]{0,1:T(8,128)(2,1)}, u32[]{:S(2)}) copy-start(bf16[3584,16]{0,1:T(8,128)(2,1)} %param.18) | copy-start | bytes 344068
  7.2 503.6 %all-gather.11.cloned.1.call-start = ((), (), s32[]{:S(2)}) async-start(), calls=%async_computation.2 | async-start | bytes 28901376 | tf_op jit(solution)/shard_map/all_gather | solution.py:25
  7.9 994.5 %all-gather.7.cloned.1.call-start = ((), (), s32[]{:S(2)}) async-start(), calls=%async_computation | async-start | bytes 28901376 | tf_op jit(solution)/shard_map/all_gather | solution.py:23
  8.7 1485.4 %all-gather.9.cloned.1.call-start = ((), (), s32[]{:S(2)}) async-start(), calls=%async_computation.1 | async-start | bytes 28901376 | tf_op jit(solution)/shard_map/all_gather | solution.py:24
  542.7 459.6 %copy-start.2 = (bf16[16,3584]{1,0:T(8,128)(2,1)S(1)}, bf16[16,3584]{1,0:T(8,128)(2,1)}, u32[]{:S(2)}) copy-start(bf16[16,3584]{1,0:T(8,128)(2,1)} %param.13) | copy-start | bytes 344068
  561.6 932.5 %copy-start.3 = (bf16[16,3584]{1,0:T(8,128)(2,1)S(1)}, bf16[16,3584]{1,0:T(8,128)(2,1)}, u32[]{:S(2)}) copy-start(bf16[16,3584]{1,0:T(8,128)(2,1)} %param.16) | copy-start | bytes 344068
  1002.4 510.5 %copy-start.1 = (bf16[3584,16]{0,1:T(8,128)(2,1)S(1)}, bf16[3584,16]{0,1:T(8,128)(2,1)}, u32[]{:S(2)}) copy-start(bf16[3584,16]{0,1:T(8,128)(2,1)} %param.18) | copy-start | bytes 344068
Sparse Core Ops, SparseCore 0:
  9.5 501.2 all-gather.10
  512.4 489.9 all-gather.6
  1003.9 490.1 all-gather.8
where the time goes:
time: 1520 us
  waiting for transfers between devices  1190 us (78%)
  blocking collectives  226 us (15%)
  matrix products  56.5 us (4%)
  local copies, waits for them, and re-layouts  32.9 us (2%)
    all_gather x1, waiting for transfers between devices, per_device(): lax.all_gather(train_up, 'fsdp', axis=0, tiled=True)  473 us
    all_gather x1, waiting for transfers between devices, per_device(): lax.all_gather(train_gate, 'fsdp', axis=0, tiled=True)  441 us
    all_gather x1, waiting for transfers between devices, per_device(): lax.all_gather(train_down, 'fsdp', axis=1, tiled=True)  273 us
    all_gather x1, blocking collectives, per_device(): lax.all_gather(low_gate, 'fsdp', axis=0, tiled=True)  70 us
    unnamed x1, blocking collectives  64.3 us
    all_gather x1, blocking collectives, per_device(): lax.all_gather(high_down, 'fsdp', axis=1, tiled=True)  48.2 us
    all_gather x1, blocking collectives, per_device(): lax.all_gather(low_up, 'fsdp', axis=0, tiled=True)  43.9 us
    all_gather x1, local copies, waits for them, and re-layouts, per_device(): lax.all_gather(train_down, 'fsdp', axis=1, tiled=True)  31.9 us
  transfers between devices with their start and end apart: 3, of which 3 were waited for; matrix products, arithmetic and copies ran while one was open for 5% of the time, Pallas kernels for 0%

commit v1 on v0

v1 whole, which is shorter than its diff:
```python
import functools

import jax
import jax.numpy as jnp
from jax import lax
from jax.experimental import pallas as pl
from jax.experimental.pallas import tpu as pltpu
from jax.sharding import PartitionSpec as P

MESH = pl.DeviceIdType.MESH
LANES = 128
SUBLANES = 16
mix_rate = 1.0


def merged(base, low, high):
    product = mix_rate * jnp.dot(low, high, preferred_element_type=jnp.float32)
    return (base.astype(jnp.float32) + product).astype(jnp.bfloat16)


def fold_of(width):
    fold = 1
    while width * fold % LANES:
        fold += 1
    return fold


def sends(k, depth, chunks):
    half = chunks // 2
    every, first, second = range(chunks), range(half), range(half, chunks)
    last = depth - 1
    down, up, side = [], [], [(k, 0, every)]
    if k > 0:
        down = [(z, 0, every) for z in range(k, depth)]
        if k == 1:
            down.append((k, 1, first))
        elif k == last:
            down.append((k, 1, every))
    if k < last:
        up = [(z, 0, every) for z in range(k, -1, -1)]
        if k == last - 1:
            up.append((k, 1, first))
        elif k == 0:
            up.append((k, 1, every))
    for z in sorted(set(range(depth)) - {k}, key=lambda z: abs(z - k)):
        if (k == 0 and z == 1) or (k == last and z == last - 1):
            side.append((z, 0, second))
        elif not (0 < k < last and ((k == 1 and z == 0) or (k == last - 1 and z == last))):
            side.append((z, 0, every))
    return [[(z, row, c) for z, row, cs in runs for c in cs] for runs in (down, up, side)]


def receives(k, depth, chunks):
    down = sends(k + 1, depth, chunks)[0] if k < depth - 1 else []
    up = sends(k - 1, depth, chunks)[1] if k > 0 else []
    side = [(z, 1 - row, c) for z, row, c in sends(k, depth, chunks)[2]]
    return [down, up, side]


def plan(k, depth, chunks):
    outs, ins = sends(k, depth, chunks), receives(k, depth, chunks)
    arrives = {item: (slot, s) for s, items in enumerate(ins) for slot, item in enumerate(items)}
    order = []
    for s, items in enumerate(outs):
        key = 0
        for slot, item in enumerate(items):
            if item[:2] != (k, 0):
                key = max(key, arrives[item][0] + 1, slot - 2)
            order.append((key, slot, s, item))
    return outs, ins, arrives, sorted(order)


def gather_kernel(n_fsdp, n_cols, parts, *refs):
    own = refs[:3]
    norm_ref = refs[3]
    out = refs[4:7]
    norms = refs[7]
    send_sem, recv_sem, local_sem, col_send, col_recv, row_send, row_recv = refs[8:]
    depth, chunks = n_fsdp // 2, 3 * parts
    here, col = lax.axis_index("fsdp"), lax.axis_index("cols")
    place, side = lax.div(here, 2), lax.rem(here, 2)

    barrier = pltpu.get_barrier_semaphore()
    for step in range(1, n_fsdp):
        peer = lax.rem(here + step, n_fsdp)
        pl.semaphore_signal(barrier, inc=1, device_id={"fsdp": peer}, device_id_type=MESH)
    for step in range(1, n_cols):
        peer = lax.rem(col + step, n_cols)
        pl.semaphore_signal(barrier, inc=1, device_id={"cols": peer}, device_id_type=MESH)
    pl.semaphore_wait(barrier, n_fsdp - 1 + n_cols - 1)

    def view(ref, c):
        rows = ref.shape[-2] // parts
        return pl.ds(c % parts * rows, rows)

    def landing(item):
        z, row, c = item
        block = 2 * z + (side if row == 0 else 1 - side)
        ref = out[c // parts]
        return ref.at[block, view(ref, c)]

    def source(k, item):
        z, row, c = item
        if (z, row) == (k, 0):
            ref = own[c // parts]
            return ref.at[view(ref, c)]
        return landing(item)

    def body(k):
        outs, ins, arrives, order = plan(k, depth, chunks)
        targets = (2 * (k - 1) + side, 2 * (k + 1) + side, 2 * k + 1 - side)
        waited = set()

        def copy(s, slot, item):
            return pltpu.make_async_remote_copy(
                src_ref=source(k, item),
                dst_ref=landing(item),
                send_sem=send_sem.at[s, slot],
                recv_sem=recv_sem.at[s, slot],
                device_id={"fsdp": targets[s]},
                device_id_type=MESH,
            )

        def arrive(s, slot):
            if (s, slot) in waited:
                return
            waited.add((s, slot))
            block = landing(ins[s][slot])
            pltpu.make_async_remote_copy(
                src_ref=block,
                dst_ref=block,
                send_sem=send_sem.at[s, slot],
                recv_sem=recv_sem.at[s, slot],
                device_id={"fsdp": targets[2]},
                device_id_type=MESH,
            ).wait_recv()

        for _, slot, s, item in order:
            if item[:2] != (k, 0):
                at, stream = arrives[item]
                arrive(stream, at)
            copy(s, slot, item).start()
        for slot in range(max(len(items) for items in ins)):
            for s in range(3):
                if slot < len(ins[s]):
                    arrive(s, slot)
        for s in range(3):
            for slot, item in enumerate(outs[s]):
                copy(s, slot, item).wait_send()

    mine = pltpu.make_async_copy(norm_ref, norms.at[here, col], local_sem.at[3])
    mine.start()
    for step in range(1, n_cols):
        pltpu.make_async_remote_copy(
            src_ref=norm_ref,
            dst_ref=norms.at[here, col],
            send_sem=col_send.at[step],
            recv_sem=col_recv.at[step],
            device_id={"cols": lax.rem(col + step, n_cols)},
            device_id_type=MESH,
        ).start()
    mine.wait()
    for step in range(1, n_cols):
        pltpu.make_async_remote_copy(
            src_ref=norm_ref,
            dst_ref=norms.at[here, lax.rem(col + n_cols - step, n_cols)],
            send_sem=col_send.at[step],
            recv_sem=col_recv.at[step],
            device_id={"cols": lax.rem(col + step, n_cols)},
            device_id_type=MESH,
        ).wait()

    def row_copy(step, block):
        return pltpu.make_async_remote_copy(
            src_ref=norms.at[here],
            dst_ref=norms.at[block],
            send_sem=row_send.at[step],
            recv_sem=row_recv.at[step],
            device_id={"fsdp": lax.rem(here + step, n_fsdp)},
            device_id_type=MESH,
        )

    for step in range(1, n_fsdp):
        row_copy(step, here).start()

    local = [pltpu.make_async_copy(own[a], out[a].at[here], local_sem.at[a]) for a in range(3)]
    for c in local:
        c.start()
    for k in range(depth):
        pl.when(place == k)(functools.partial(body, k))
    for c in local:
        c.wait()
    for step in range(1, n_fsdp):
        row_copy(step, lax.rem(here + n_fsdp - step, n_fsdp)).wait()


def gather(n_fsdp, n_cols, pieces, norm):
    parts = 2 if n_fsdp <= 8 else 1
    slots = 3 * parts * n_fsdp // 2
    anywhere = pl.BlockSpec(memory_space=pl.ANY)
    dma = pltpu.SemaphoreType.DMA
    return pl.pallas_call(
        functools.partial(gather_kernel, n_fsdp, n_cols, parts),
        out_shape=[jax.ShapeDtypeStruct((n_fsdp,) + p.shape, p.dtype) for p in pieces]
        + [jax.ShapeDtypeStruct((n_fsdp, n_cols) + norm.shape, norm.dtype)],
        in_specs=[anywhere] * 4,
        out_specs=[anywhere] * 4,
        scratch_shapes=[
            dma((3, slots)),
            dma((3, slots)),
            dma((4,)),
            dma((n_cols,)),
            dma((n_cols,)),
            dma((n_fsdp,)),
            dma((n_fsdp,)),
        ],
        compiler_params=pltpu.CompilerParams(collective_id=0, has_side_effects=True),
    )(*pieces, norm)


def unfold_kernel(fold, in_ref, out_ref):
    width = in_ref.shape[-1] // fold
    for p in range(fold):
        out_ref[p] = jnp.concatenate(
            [in_ref[0, j, :, p * width : (p + 1) * width] for j in range(fold)], axis=1
        )


def unfold(blocks, fold):
    count, rows, width = blocks.shape
    tile = next(t for t in (448, 224, 112, 16) if rows % t == 0)
    out = pl.pallas_call(
        functools.partial(unfold_kernel, fold),
        grid=(count // fold, rows // tile),
        out_shape=jax.ShapeDtypeStruct((fold, rows, count // fold * width), blocks.dtype),
        in_specs=[pl.BlockSpec((1, fold, tile, width), lambda z, r: (z, 0, r, 0))],
        out_specs=pl.BlockSpec((fold, tile, width), lambda z, r: (0, r, z)),
    )(blocks.reshape(count // fold, fold, rows, width))
    return out.reshape(fold * rows, -1)


def per_device(
    n_fsdp,
    n_cols,
    train_gate,
    low_gate,
    high_gate,
    train_up,
    low_up,
    high_up,
    train_down,
    low_down,
    high_down,
    norm_train,
    norm_step,
):
    gate = merged(train_gate, low_gate, high_gate)
    up = merged(train_up, low_up, high_up)
    down = merged(train_down, low_down, high_down)
    rows, width = down.shape
    fold = fold_of(width)
    down = jnp.concatenate(jnp.split(down, fold, axis=0), axis=1)
    length = norm_train.shape[0]
    norm = jnp.pad(norm_train + norm_step, (0, -length % LANES))
    norm = jnp.broadcast_to(norm[None], (8, norm.shape[0]))
    gates, ups, downs, norms = gather(n_fsdp, n_cols, (gate, up, down), norm)
    serve_norm = norms[:, :, 0, :length].reshape(-1).astype(jnp.bfloat16)
    return (
        gates.reshape(-1, gates.shape[-1]),
        ups.reshape(-1, ups.shape[-1]),
        unfold(downs, fold),
        serve_norm,
    )


def solution(mesh):
    return jax.shard_map(
        functools.partial(per_device, mesh.shape["fsdp"], mesh.shape["cols"]),
        mesh=mesh,
        in_specs=(
            P("fsdp", "cols"),
            P("fsdp", None),
            P(None, "cols"),
            P("fsdp", "cols"),
            P("fsdp", None),
            P(None, "cols"),
            P("cols", "fsdp"),
            P("cols", None),
            P(None, "fsdp"),
            P(("fsdp", "cols")),
            P(("fsdp", "cols")),
        ),
        out_specs=(P(None, "cols"), P(None, "cols"), P("cols", None), P()),
        check_vma=False,
    )
```

time: 1520 us -> 819 us (0.54)
  waiting for transfers between devices: 1190 us -> 0 us
  Pallas kernels: 0 us -> 762 us
  blocking collectives: 226 us -> 0 us
  matrix products: 56.5 us -> 11.6 us
    all_gather x3 -> x0, waiting for transfers between devices: 1190 us -> none  [the longest x1 473 us: per_device(): lax.all_gather(train_up, 'fsdp', axis=0, tiled=True)]
    pallas_call x0 -> x2, Pallas kernels: none -> 762 us  [the longest x1 738 us: gather(): pl.pallas_call(functools.partial(gather_kernel, n_fsdp, n_cols, parts), o...]
    all_gather x3 -> x0, blocking collectives: 162 us -> none  [the longest x1 70 us: per_device(): lax.all_gather(low_gate, 'fsdp', axis=0, tiled=True)]
    unnamed x1 -> x0, blocking collectives: 64.3 us -> none
    dot_general x3, matrix products: 56.5 us -> 11.6 us  [merged(): product = mix_rate * jnp.dot(low, high, preferred_element_type=jnp.float32)]
    unnamed x13 -> x20, local copies, waits for them, and re-layouts: 0.71 us -> 34.4 us
    all_gather x4 -> x0, local copies, waits for them, and re-layouts: 32.2 us -> none  [the longest x1 31.9 us: per_device(): lax.all_gather(train_down, 'fsdp', axis=1, tiled=True)]
  transfers between devices with their start and end apart: 3 -> 0, of which waited for: 3 -> 0; matrix products, arithmetic and copies ran while one was open for 5% -> 0% of each run, Pallas kernels for 0% -> 0%
where the time goes in v1:
time: 819 us
  Pallas kernels  762 us (93%)
  local copies, waits for them, and re-layouts  41.2 us (5%)
  matrix products  11.6 us (1%)
    pallas_call x1, Pallas kernels, gather(): pl.pallas_call(functools.partial(gather_kernel, n_fsdp, n_cols, parts), o...  738 us
    unnamed x20, local copies, waits for them, and re-layouts  34.4 us
    pallas_call x1, Pallas kernels, unfold(): pl.pallas_call(functools.partial(unfold_kernel, fold), grid=(count // fol...  24.3 us

profile of v1, /device:TPU:0, one launch (start us, length us, event | category | flops | bytes accessed | tf_op | source)
XLA Modules:
  0.0 818.9 jit_solution(14646733159235674585)
XLA Ops:
  0.6 0.0 copy-start
  0.6 0.0 copy-start.6
  0.7 0.0 copy-start.7
  0.7 0.0 copy-start.3
  0.7 0.8 add.17
  1.5 0.6 broadcast_in_dim.2.refs_3_
  2.1 0.0 copy-done
  2.1 4.6 add_convert_fusion.2.refs_0_
  6.7 0.0 copy-done.6
  6.7 0.0 copy-done.7
  6.8 0.0 copy-done.3
  6.8 0.0 copy-start.4
  6.8 2.7 add_convert_fusion.1.refs_1_
  9.5 0.0 copy-done.4
  9.5 0.0 copy-start.5
  9.5 0.0 copy-start.8
  9.5 4.3 copy.19
  13.8 0.0 copy-done.5
  13.8 0.0 copy-done.8
  13.8 4.2 add_convert_fusion
  18.0 0.2 fusion.1
  18.2 2.7 pad_maximum_fusion.refs_2_
  21.0 737.7 %shard_map.138 = (bf16[8,448,3584]{2,1,0:T(8,128)(2,1)}, bf16[8,448,3584]{2,1,0:T(8,128)(2,1)}, bf16[8,1792,896]{2,1,0:T(8,128)(2,1)}, f32[8,4,8,128]{3,2,1,0:T(8,128)}) custom-call(bf16[448,3584]{1,0:T(8,128)(2,1)} %add_convert_fusion.2.refs_0_, bf16[448,3584]{1,0:T(8,128)(2,1)} %add_convert_fusion.1.refs_1_, bf16[1792,896]{1,0:T(8,128)(2,1)} %pad_maximum_fusion.refs_2_, ...), custom_call_target="tpu_custom_call" | custom-call | tf_op jit(solution)/shard_map/pallas_call | solution.py:202
  758.6 1.0 fusion
  759.6 0.7 convert_element_type.30
  760.3 24.3 %shard_map.139 = bf16[2,1792,3584]{2,1,0:T(8,128)(2,1)} custom-call(bf16[4,2,1792,896]{3,2,1,0:T(8,128)(2,1)} %bitcast.13), custom_call_target="tpu_custom_call" | custom-call | tf_op jit(solution)/shard_map/pallas_call | solution.py:232
  784.5 0.0 copy-start.2
  784.5 22.1 %copy.24 = bf16[3584,3584]{1,0:T(8,128)(2,1)} copy(bf16[3584,3584]{1,0:T(8,128)(2,1)} %bitcast.12) | data formatting | bytes 51380224
  806.6 3.2 copy-done.2
  809.9 0.0 copy-start.1
  809.9 9.1 %copy.25 = bf16[3584,3584]{1,0:T(8,128)(2,1)} copy(bf16[3584,3584]{1,0:T(8,128)(2,1)S(1)} %bitcast.11) | data formatting | bytes 51380224
  818.9 0.0 copy-done.1
  (1 shorter events, 0.0 us)
Async XLA Ops:
  0.6 1.5 copy-start
  0.6 6.1 copy-start.6
  0.7 6.1 copy-start.7
  0.7 6.1 copy-start.3
  6.8 2.7 copy-start.4
  9.5 4.3 copy-start.5
  9.5 4.3 copy-start.8
  784.5 25.3 %copy-start.2 = (bf16[8,448,3584]{2,1,0:T(8,128)(2,1)S(1)}, bf16[8,448,3584]{2,1,0:T(8,128)(2,1)}, u32[]{:S(2)}) copy-start(bf16[8,448,3584]{2,1,0:T(8,128)(2,1)} %get-tuple-element.9) | copy-start | bytes 77070336
  809.9 9.1 %copy-start.1 = (bf16[16,3584]{1,0:T(8,128)(2,1)S(1)}, bf16[16,3584]{1,0:T(8,128)(2,1)}, u32[]{:S(2)}) copy-start(bf16[16,3584]{1,0:T(8,128)(2,1)} %param.13) | copy-start | bytes 344068
